TPU v7x, 32 devices: a whole 2x2x4 slice. The times are simulated.
32 devices in a mesh: pipe: 4 (over x, core), vocab: 8 (over z, y).
Axes of the slice: x: 2, y: 2, z: 4, core: 2. Of those that a mesh axis runs over, the one named last changes fastest.
Arguments:
- hidden: bfloat16 [4, 128, 4096], P('pipe'), may hold values from -60 to 60
- norm_gain: float32 [4096], replicated, may hold values from 0.5 to 1.5
- out_weight: bfloat16 [128256, 4096], P(('pipe', 'vocab')), may hold values from -4 to 4
- targets: int32 [4, 128], P('pipe'), may hold values from 0 to 128255
- loss_mask: int32 [4, 128], P('pipe'), may hold values from 0 to 1, as said below
- slot_position: int32 [4, 128], P('pipe'), may hold values from 0 to 127, each once within a row
- counts: int32 [4], replicated, may hold values from 1 to 128, 320 in all
- loss_scale: float32 [], replicated, may hold values from 4096 to 32768
Outputs:
- loss: float32 [], replicated
- grad_hidden: bfloat16 [4, 128, 4096], P('pipe')
Inputs may be any that keep to these rules, and one draw needn't show every extreme that they name: The 4 counts sum to exactly 320, and one of them equals 128. Each row of slot_position holds every number of 0 to 127 once. Each row of loss_mask holds at least 64 ones.
All inputs are finite; a program needn't handle non-finite values.
Results may differ from a plain program's by a relative error of at most 0.0034.
Values may be sent and summed in bfloat16 or wider, within the bound.
A program may use at most 128 MiB of HBM per device.

v0:
```python
import jax
import jax.numpy as jnp
from jax import lax
from jax.sharding import PartitionSpec as P

EPSILON = 1e-05


def rms_scale(values, norm_gain):
    mean_square = jnp.mean(values * values, axis=-1, keepdims=True)
    return values * lax.rsqrt(mean_square + EPSILON) * norm_gain


def pull_rows(rows, norm_gain, cotangent):
    pullback = jax.vjp(lambda values: rms_scale(values, norm_gain), rows)[1]
    return pullback(cotangent)[0].astype(jnp.bfloat16)


def softmax_stats(logits, local_target):
    row_top = lax.pmax(jnp.max(logits, axis=1), ("pipe", "vocab"))
    local_total = jnp.sum(jnp.exp(logits - row_top[:, None]), axis=1)
    exp_total, target_logit = lax.psum((local_total, local_target), ("pipe", "vocab"))
    return (row_top + jnp.log(exp_total), target_logit)


def body(hidden, norm_gain, out_weight, targets, loss_mask, slot_position, counts, loss_scale):
    micro_slots = hidden.shape[1]
    model_width = hidden.shape[2]
    shard_words = out_weight.shape[0]
    offset = lax.axis_index(("pipe", "vocab")) * shard_words
    own_rows = hidden.reshape(micro_slots, model_width).astype(jnp.float32)
    own_normed = rms_scale(own_rows, norm_gain).astype(jnp.bfloat16)
    all_normed, all_targets, all_masks, all_positions = (
        lax.all_gather(own_normed, "pipe", axis=0, tiled=True),
        lax.all_gather(targets.reshape(micro_slots), "pipe", axis=0, tiled=True),
        lax.all_gather(loss_mask.reshape(micro_slots), "pipe", axis=0, tiled=True),
        lax.all_gather(slot_position.reshape(micro_slots), "pipe", axis=0, tiled=True),
    )
    rows_total = all_normed.shape[0]
    micro_index = jnp.arange(rows_total, dtype=jnp.int32) // micro_slots
    count_row = jnp.sum(
        jnp.where(
            micro_index[:, None] == jnp.arange(counts.shape[0], dtype=jnp.int32)[None, :],
            counts[None, :],
            0,
        ),
        axis=1,
    )
    inside = all_positions < count_row
    token_weight = jnp.where(inside & (all_masks == 1), 1.0, 0.0).astype(jnp.float32)
    weight_total = jnp.sum(token_weight)
    work_normed, work_targets, work_weight = (all_normed, all_targets, token_weight)
    logits = lax.dot_general(
        work_normed, out_weight, (((1,), (1,)), ((), ())), preferred_element_type=jnp.float32
    )
    is_target = (
        jnp.arange(shard_words, dtype=jnp.int32)[None, :] == (work_targets - offset)[:, None]
    )
    local_target = jnp.sum(jnp.where(is_target, logits, 0.0), axis=1)
    log_total, target_logit = softmax_stats(logits, local_target)
    loss = jnp.sum(work_weight * (log_total - target_logit)) / weight_total
    token_coef = loss_scale * work_weight / weight_total
    logit_grad = (
        (jnp.exp(logits - log_total[:, None]) - is_target.astype(jnp.float32)) * token_coef[:, None]
    ).astype(jnp.bfloat16)
    work_grad = jnp.dot(logit_grad, out_weight, preferred_element_type=jnp.float32)
    grad_cube = work_grad.reshape(rows_total // micro_slots, micro_slots, model_width)
    micro_grad = lax.psum_scatter(grad_cube, "pipe", scatter_dimension=0, tiled=True)
    summed = lax.psum(micro_grad, "vocab")
    grad_out = pull_rows(own_rows, norm_gain, summed.reshape(micro_slots, model_width))
    return (loss, grad_out.reshape(1, micro_slots, model_width))


def solution(mesh):
    in_specs = (
        P("pipe", None, None),
        P(),
        P(("pipe", "vocab"), None),
        P("pipe", None),
        P("pipe", None),
        P("pipe", None),
        P(),
        P(),
    )
    out_specs = (P(), P("pipe", None, None))
    return jax.shard_map(body, mesh=mesh, in_specs=in_specs, out_specs=out_specs, check_vma=False)
```

profile of v0, /device:TPU:0, one launch (start us, length us, event | category | flops | bytes accessed | tf_op | source)
XLA Modules:
  0.0 372.7 jit_solution(8846889576664135234)
XLA Ops:
  7.2 0.0 all-gather.5.cloned.1.call-start
  7.3 1.5 fusion.7
  8.8 2.5 fusion.9
  11.3 0.0 all-gather.5.cloned.1.call-update
  11.3 0.0 reduce-scatter.2.cloned.1.call-start
  12.0 6.0 %all-gather.2 = s32[1,512]{1,0:T(1,128)S(1)} all-gather(s32[1,128]{1,0:T(1,128)S(1)} %copy-done.3), channel_id=4, replica_groups=mesh['pipe'=4,'vocab'=8] {'pipe'}, dimensions={1}, use_global_device_ids=true | all-gather | bytes 2560 | tf_op jit(solution)/shard_map/all_gather | solution.py:35
  18.1 5.4 %all-gather.1 = s32[1,512]{1,0:T(1,128)S(1)} all-gather(s32[1,128]{1,0:T(1,128)S(1)} %copy-done.4), channel_id=3, replica_groups=mesh['pipe'=4,'vocab'=8] {'pipe'}, dimensions={1}, use_global_device_ids=true | all-gather | bytes 2560 | tf_op jit(solution)/shard_map/all_gather | solution.py:36
  23.4 5.2 %all-gather = s32[1,512]{1,0:T(1,128)S(1)} all-gather(s32[1,128]{1,0:T(1,128)S(1)} %copy-done.5), channel_id=2, replica_groups=mesh['pipe'=4,'vocab'=8] {'pipe'}, dimensions={1}, use_global_device_ids=true | all-gather | bytes 2560 | tf_op jit(solution)/shard_map/all_gather | solution.py:37
  28.6 0.1 select_reduce_fusion.1
  28.7 19.9 %all-gather.5.cloned.1.call-done = bf16[512,4096]{1,0:T(8,128)(2,1)} async-done(((bf16[128,4096]{1,0:T(8,128)(2,1)}), bf16[512,4096]{1,0:T(8,128)(2,1)}) %all-gather.5.cloned.1.call-update) | async-done | bytes 4194320 | tf_op jit(solution)/shard_map/all_gather | solution.py:34
  48.7 23.8 %fusion.18 = (f32[512]{0:T(512)S(1)}, f32[512,4008]{0,1:T(8,128)}) fusion(bf16[512,4096]{1,0:T(8,128)(2,1)} %all-gather.5.cloned.1.call-done, bf16[4008,4096]{1,0:T(8,128)(2,1)} %param.10), kind=kOutput, calls=%fused_computation.41 | convolution fusion | flops 16812822528 | bytes 45238272 | tf_op jit(solution)/shard_map/dot_general | solution.py:53
  72.4 39.2 %pmax.7 = f32[512]{0:T(512)S(1)} all-reduce(f32[512]{0:T(512)S(1)} %get-tuple-element.10), channel_id=1, replica_groups=mesh['pipe'=4,'vocab'=8] {'pipe','vocab'}, use_global_device_ids=true, to_apply=%region_3.4 | all-reduce | flops 512 | bytes 4096 | tf_op jit(solution)/shard_map/pmax | solution.py:20
  111.7 4.5 %select_reduce_fusion = (f32[512]{0:T(512)S(1)}, f32[512]{0:T(512)S(1)}) fusion(f32[512,4008]{0,1:T(8,128)} %get-tuple-element.11, s32[512]{0:T(512)S(1)} %bitcast.27, f32[512]{0:T(512)S(1)} %pmax.7), kind=kLoop, calls=%fused_computation.1 | loop fusion | flops 10259456 | bytes 8216576 | tf_op jit(solution)/shard_map/reduce_sum | solution.py:59
  116.2 41.0 %all-reduce = (f32[512]{0:T(512)S(1)}, f32[512]{0:T(512)S(1)}) all-reduce(f32[512]{0:T(512)S(1)} %get-tuple-element.3, f32[512]{0:T(512)S(1)} %get-tuple-element.2), channel_id=1, replica_groups=mesh['pipe'=4,'vocab'=8] {'pipe','vocab'}, use_global_device_ids=true, to_apply=%region_5.6 | all-reduce | flops 1024 | bytes 8192 | tf_op jit(solution)/shard_map/psum | solution.py:22
  157.1 0.6 select_reduce_fusion.2
  157.8 0.7 fusion.13
  158.4 25.5 %fusion = f32[512,4096]{1,0:T(8,128)} fusion(bf16[4008,4096]{1,0:T(8,128)(2,1)} %param.10, f32[512,4008]{0,1:T(8,128)} %get-tuple-element.11, f32[512]{0:T(512)S(1)} %fusion.13, f32[512]{0:T(512)S(1)} %get-tuple-element.8, s32[512]{0:T(512)S(1)} %bitcast.28), kind=kOutput, calls=%fused_computation.4 | convolution fusion | flops 16823083008 | bytes 49436672 | tf_op jit(solution)/shard_map/dot_general | solution.py:66
  183.9 0.0 reduce-scatter.2.cloned.1.call-update
  184.0 0.0 all-reduce.3.cloned.1.call-start
  184.0 71.2 %reduce-scatter.2.cloned.1.call-done = f32[1,128,4096]{2,1,0:T(8,128)} async-done(((f32[4,128,4096]{2,1,0:T(8,128)}), f32[1,128,4096]{2,1,0:T(8,128)}) %reduce-scatter.2.cloned.1.call-update) | async-done | bytes 2097168 | tf_op jit(solution)/shard_map/reduce_scatter | solution.py:68
  256.6 104.7 %all-reduce.3.cloned.1.call-done = f32[1,128,4096]{2,1,0:T(8,128)} async-done(((f32[1,128,4096]{2,1,0:T(8,128)}), f32[1,128,4096]{2,1,0:T(8,128)}) %all-reduce.3.cloned.1.call-update) | async-done | bytes 2097168 | tf_op jit(solution)/shard_map/psum | solution.py:69
  361.3 2.1 fusion.10
  363.4 0.1 copy-done.1
  363.5 1.5 fusion.11
  (19 shorter events, 0.1 us)
Async XLA Ops:
  7.2 4.9 %copy-start.3 = (s32[1,128]{1,0:T(1,128)S(1)}, s32[1,128]{1,0:T(1,128)}, u32[]{:S(2)}) copy-start(s32[1,128]{1,0:T(1,128)} %param.11) | copy-start | bytes 1540
  7.2 10.9 %copy-start.4 = (s32[1,128]{1,0:T(1,128)S(1)}, s32[1,128]{1,0:T(1,128)}, u32[]{:S(2)}) copy-start(s32[1,128]{1,0:T(1,128)} %param.12) | copy-start | bytes 1540
  7.2 16.2 %copy-start.5 = (s32[1,128]{1,0:T(1,128)S(1)}, s32[1,128]{1,0:T(1,128)}, u32[]{:S(2)}) copy-start(s32[1,128]{1,0:T(1,128)} %param.13) | copy-start | bytes 1540
  7.2 21.4 %copy-start.6 = (s32[4]{0:T(128)S(1)}, s32[4]{0:T(128)}, u32[]{:S(2)}) copy-start(s32[4]{0:T(128)} %param.14) | copy-start | bytes 52
  7.2 41.5 %all-gather.5.cloned.1.call-start = ((), (), s32[]{:S(2)}) async-start(), calls=%async_computation.1 | async-start | bytes 5242880 | tf_op jit(solution)/shard_map/all_gather | solution.py:34
  11.3 243.9 %reduce-scatter.2.cloned.1.call-start = ((), (), s32[]{:S(2)}) async-start(), calls=%async_computation.2 | async-start | bytes 10485760 | tf_op jit(solution)/shard_map/reduce_scatter | solution.py:68
  183.9 177.3 %copy-start = (bf16[1,128,4096]{2,1,0:T(8,128)(2,1)S(1)}, bf16[1,128,4096]{2,1,0:T(8,128)(2,1)}, u32[]{:S(2)}) copy-start(bf16[1,128,4096]{2,1,0:T(8,128)(2,1)} %param.8) | copy-start | bytes 3145732
  183.9 177.3 %copy-start.2 = (f32[4096]{0:T(1024)S(1)}, f32[4096]{0:T(1024)}, u32[]{:S(2)}) copy-start(f32[4096]{0:T(1024)} %param.9) | copy-start | bytes 49156
  184.0 177.3 %all-reduce.3.cloned.1.call-start = ((), (), s32[]{:S(2)}) async-start(), calls=%async_computation.3 | async-start | bytes 4194304 | tf_op jit(solution)/shard_map/psum | solution.py:69
  361.3 2.2 copy-start.1
Sparse Core Ops, SparseCore 0:
  11.5 37.1 all-gather.4
  184.1 71.1 reduce-scatter.1
  258.9 102.3 all-reduce.2
where the time goes:
time: 373 us
  waiting for transfers between devices  196 us (53%)
  blocking collectives  96.8 us (26%)
  matrix products  49.3 us (13%)
  between operations  16.9 us (5%)
  other arithmetic  13.6 us (4%)
    psum x1, waiting for transfers between devices, body(): summed = lax.psum(micro_grad, 'vocab')  105 us
    reduce_scatter x1, waiting for transfers between devices, body(): lax.psum_scatter(grad_cube, 'pipe', scatter_dimension=0, tiled=True)  71.2 us
    psum x1, blocking collectives, softmax_stats(): lax.psum((local_total, local_target), ('pipe', 'vocab'))  41 us
    pmax x1, blocking collectives, softmax_stats(): row_top = lax.pmax(jnp.max(logits, axis=1), ('pipe', 'vocab'))  39.2 us
    dot_general x1, matrix products, body(): jnp.dot(logit_grad, out_weight, preferred_element_type=jnp.float32)  25.5 us
    dot_general x1, matrix products, body(): lax.dot_general(work_normed, out_weight, (((1,), (1,)), ((), ())), prefer...  23.8 us
    all_gather x1, waiting for transfers between devices, body(): lax.all_gather(own_normed, 'pipe', axis=0, tiled=True)  19.9 us
  transfers between devices with their start and end apart: 3, of which 3 were waited for; matrix products, arithmetic and copies ran while one was open for 0% of the time, Pallas kernels for 0%

commit v1 on v0

v1 whole, which is shorter than its diff:
```python
import functools
import jax
import jax.numpy as jnp
from jax import lax
from jax.experimental import pallas as pl
from jax.experimental.pallas import tpu as pltpu
from jax.sharding import PartitionSpec as P

EPSILON = 1e-05
MESH = pl.DeviceIdType.MESH
F32 = jnp.float32
BF16 = jnp.bfloat16
VMEM = pl.BlockSpec(memory_space=pltpu.VMEM)


def rms_scale(values, norm_gain):
    mean_square = jnp.mean(values * values, axis=-1, keepdims=True)
    return values * lax.rsqrt(mean_square + EPSILON) * norm_gain


def pull_rows(rows, norm_gain, cotangent):
    pullback = jax.vjp(lambda values: rms_scale(values, norm_gain), rows)[1]
    return pullback(cotangent)[0].astype(BF16)


def place(ny):
    p, v = lax.axis_index("pipe"), lax.axis_index("vocab")
    return p // 2, p % 2, v % ny, v // ny


def greet(targets):
    barrier = pltpu.get_barrier_semaphore()
    for target in targets:
        pl.semaphore_signal(barrier, inc=1, device_id=target, device_id_type=MESH)
    pl.semaphore_wait(barrier, len(targets))


def remote(src, dst, send, recv, target):
    return pltpu.make_async_remote_copy(
        src_ref=src, dst_ref=dst, send_sem=send, recv_sem=recv,
        device_id=target, device_id_type=MESH,
    )


def gather_kernel(ny, chunks, own, ints, out, oints, sems_s, sems_r, own_s, own_r, int_s, int_r):
    x, core, y, z = place(ny)
    p, v = x * 2 + core, z * ny + y
    mate = (x * 2 + (1 - core), v)
    across = ((1 - x) * 2 + core, v)
    diag = ((1 - x) * 2 + (1 - core), v)
    beside = (p, z * ny + (1 - y))
    greet([mate, across, diag, beside])
    far = (1 - x) * 2 + core
    started = []
    first = []
    for c in range(chunks):
        cp = remote(own.at[y, c], out.at[p, y, c], sems_s.at[0, c], sems_r.at[0, c], across)
        cp.start()
        first.append(cp)
    for j, target in enumerate((mate, across, diag)):
        cp = remote(ints, oints.at[p], int_s.at[j], int_r.at[j], target)
        cp.start()
        started.append(cp)
    cp = remote(own, out.at[p], own_s, own_r, mate)
    cp.start()
    started.append(cp)
    oints[p] = ints[...]
    out[p] = own[...]
    second = []
    for c in range(chunks):
        first[c].wait_recv()
        cy = remote(out.at[far, y, c], out.at[far, y, c], sems_s.at[1, c], sems_r.at[1, c], beside)
        cy.start()
        cm = remote(out.at[far, y, c], out.at[far, y, c], sems_s.at[2, c], sems_r.at[2, c], mate)
        cm.start()
        second.append(cy)
        started.append(cm)
    for c in range(chunks):
        second[c].wait_recv()
        cm = remote(out.at[far, 1 - y, c], out.at[far, 1 - y, c], sems_s.at[3, c], sems_r.at[3, c], mate)
        cm.start()
        started.append(cm)
    for cp in started:
        cp.wait_recv()
    for cp in first + second + started:
        cp.wait_send()


def gather(own, ints, pipe, ny, chunks):
    rows, width = own.shape
    part = rows // (2 * chunks)
    out, oints = pl.pallas_call(
        functools.partial(gather_kernel, ny, chunks),
        out_shape=(
            jax.ShapeDtypeStruct((pipe, 2, chunks, part, width), BF16),
            jax.ShapeDtypeStruct((pipe,) + ints.shape, jnp.int32),
        ),
        in_specs=[VMEM, VMEM],
        out_specs=(VMEM, VMEM),
        scratch_shapes=[
            pltpu.SemaphoreType.DMA((4, chunks)),
            pltpu.SemaphoreType.DMA((4, chunks)),
            pltpu.SemaphoreType.DMA,
            pltpu.SemaphoreType.DMA,
            pltpu.SemaphoreType.DMA((3,)),
            pltpu.SemaphoreType.DMA((3,)),
        ],
        compiler_params=pltpu.CompilerParams(
            collective_id=0, has_side_effects=True, vmem_limit_bytes=24 * 2**20
        ),
    )(own.reshape(2, chunks, part, width), ints)
    return out.reshape(pipe * rows, width), oints


def stats_kernel(pipe, vocab, st, out, box, send, recv):
    p, v = lax.axis_index("pipe"), lax.axis_index("vocab")
    peers = []
    for dp in range(pipe):
        for dv in range(vocab):
            if dp or dv:
                peers.append((lax.rem(p + dp, pipe), lax.rem(v + dv, vocab)))
    greet(peers)
    copies = []
    for j, target in enumerate(peers):
        cp = remote(st, box.at[j], send.at[j], recv.at[j], target)
        cp.start()
        copies.append(cp)
    for cp in copies:
        cp.wait_recv()
    n = st.shape[1]
    own_top = st[0]
    tops = box[:, 0]
    top = jnp.maximum(own_top, jnp.max(tops, axis=0))
    total = st[1] * jnp.exp(own_top - top) + jnp.sum(
        box[:, 1] * jnp.exp(tops - top[None]), axis=0
    )
    out[0] = top + jnp.log(total)
    out[1] = st[2] + jnp.sum(box[:, 2], axis=0)
    for cp in copies:
        cp.wait_send()


def combine_stats(top, total, target, pipe, vocab):
    rows = top.shape[0]
    st = jnp.stack([top, total, target]).reshape(3, rows // 128, 128)
    n = pipe * vocab - 1
    out = pl.pallas_call(
        functools.partial(stats_kernel, pipe, vocab),
        out_shape=jax.ShapeDtypeStruct((2, rows // 128, 128), F32),
        in_specs=[VMEM],
        out_specs=VMEM,
        scratch_shapes=[
            pltpu.VMEM((n,) + st.shape, F32),
            pltpu.SemaphoreType.DMA((n,)),
            pltpu.SemaphoreType.DMA((n,)),
        ],
        compiler_params=pltpu.CompilerParams(collective_id=1, has_side_effects=True),
    )(st)
    return out[0].reshape(rows), out[1].reshape(rows)


def reduce_kernel(ny, nz, g, h, gain, out, ra, sb1, sb2, rb1, rb2, sc1, sc2, rc1, rc2,
                  u, sd, rd, s_a, r_a, s_b, r_b, s_c, r_c, s_d, r_d, s_e, r_e, s_f, r_f):
    x, core, y, z = place(ny)
    p, v = x * 2 + core, z * ny + y
    half = g.shape[-1] // 2
    lo, hi = pl.ds(0, half), pl.ds(half, half)
    mate = (x * 2 + (1 - core), v)
    across = ((1 - x) * 2 + core, v)
    beside = (p, z * ny + (1 - y))
    along = [(p, lax.rem(z + d, nz) * ny + y) for d in range(1, nz)]
    greet([mate, across, beside] + along)
    copies = []

    def go(src, dst, send, recv, target):
        cp = remote(src, dst, send, recv, target)
        cp.start()
        copies.append(cp)
        return cp

    order = ((1 - x, 1 - y), (1 - x, y), (x, 1 - y), (x, y))
    pa = [go(g.at[a, 1 - core, b], ra.at[a, b], s_a.at[j], r_a.at[j], mate)
          for j, (a, b) in enumerate(order)]

    def fill(dst, i, a, b, cols):
        def one(k, carry):
            dst[i, k] = (g[a, core, b, k, :, cols] + ra[a, b, k, :, cols]).astype(BF16)
            return carry
        lax.fori_loop(0, nz, one, 0)

    pa[0].wait_recv()
    fill(sb1, 1 - y, 1 - x, 1 - y, lo)
    b10 = go(sb1.at[1 - y], rb1.at[1 - y], s_b.at[0], r_b.at[0], across)
    fill(sb2, 1 - x, 1 - x, 1 - y, hi)
    b20 = go(sb2.at[1 - x], rb2.at[1 - x], s_b.at[1], r_b.at[1], beside)
    pa[1].wait_recv()
    fill(sb1, y, 1 - x, y, lo)
    b11 = go(sb1.at[y], rb1.at[y], s_b.at[2], r_b.at[2], across)
    pa[2].wait_recv()
    fill(sb2, x, x, 1 - y, hi)
    b21 = go(sb2.at[x], rb2.at[x], s_b.at[3], r_b.at[3], beside)
    pa[3].wait_recv()

    b10.wait_recv()

    def fc1(k, carry):
        sc1[k] = (g[x, core, 1 - y, k, :, lo] + ra[x, 1 - y, k, :, lo]
                  + rb1[1 - y, k].astype(F32)).astype(BF16)
        return carry
    lax.fori_loop(0, nz, fc1, 0)
    b20.wait_recv()

    def fc2(k, carry):
        sc2[k] = (g[1 - x, core, y, k, :, hi] + ra[1 - x, y, k, :, hi]
                  + rb2[1 - x, k].astype(F32)).astype(BF16)
        return carry
    lax.fori_loop(0, nz, fc2, 0)
    c1 = go(sc1, rc1, s_c.at[0], r_c.at[0], beside)
    c2 = go(sc2, rc2, s_c.at[1], r_c.at[1], across)
    b11.wait_recv()
    b21.wait_recv()
    c1.wait_recv()
    c2.wait_recv()

    def fu(k, carry):
        a = (g[x, core, y, k, :, lo] + ra[x, y, k, :, lo]
             + rb1[y, k].astype(F32) + rc1[k].astype(F32))
        b = (g[x, core, y, k, :, hi] + ra[x, y, k, :, hi]
             + rb2[x, k].astype(F32) + rc2[k].astype(F32))
        u[k, :, lo] = a
        u[k, :, hi] = b
        sd[k, :, lo] = a.astype(BF16)
        sd[k, :, hi] = b.astype(BF16)
        return carry
    lax.fori_loop(0, nz, fu, 0)
    pd = [go(sd.at[lax.rem(z + d, nz)], rd.at[d - 1], s_d.at[d - 1], r_d.at[d - 1], along[d - 1])
          for d in range(1, nz)]
    rows = h[y, z].astype(F32)
    scale = lax.rsqrt(jnp.mean(rows * rows, axis=-1, keepdims=True) + EPSILON)
    for cp in pd:
        cp.wait_recv()
    total = u[z]
    for d in range(1, nz):
        total = total + rd[d - 1].astype(F32)
    gg = total * gain[...]
    dot = jnp.mean(rows * gg, axis=-1, keepdims=True)
    out[y, z] = (scale * gg - (scale * scale * scale) * rows * dot).astype(BF16)

    tail = [go(out.at[y, z], out.at[y, z], s_f.at[0], r_f.at[0], beside)]
    pe = [go(out.at[y, z], out.at[y, z], s_e.at[d - 1], r_e.at[d - 1], along[d - 1])
          for d in range(1, nz)]
    for d in range(1, nz):
        pe[d - 1].wait_recv()
        zz = lax.rem(z + nz - d, nz)
        tail.append(go(out.at[y, zz], out.at[y, zz], s_f.at[d], r_f.at[d], beside))
    for cp in tail:
        cp.wait_recv()
    for cp in copies:
        cp.wait_send()


def reduce_finish(grad, rows, norm_gain, ny, nz):
    micro, width = rows.shape
    part = micro // (ny * nz)
    half = width // 2
    dma = pltpu.SemaphoreType.DMA
    out = pl.pallas_call(
        functools.partial(reduce_kernel, ny, nz),
        out_shape=jax.ShapeDtypeStruct((ny, nz, part, width), BF16),
        in_specs=[VMEM] * 3,
        out_specs=VMEM,
        scratch_shapes=[
            pltpu.VMEM((2, ny, nz, part, width), F32),
            pltpu.VMEM((ny, nz, part, half), BF16),
            pltpu.VMEM((2, nz, part, half), BF16),
            pltpu.VMEM((ny, nz, part, half), BF16),
            pltpu.VMEM((2, nz, part, half), BF16),
            pltpu.VMEM((nz, part, half), BF16),
            pltpu.VMEM((nz, part, half), BF16),
            pltpu.VMEM((nz, part, half), BF16),
            pltpu.VMEM((nz, part, half), BF16),
            pltpu.VMEM((nz, part, width), F32),
            pltpu.VMEM((nz, part, width), BF16),
            pltpu.VMEM((nz - 1, part, width), BF16),
            dma((4,)), dma((4,)), dma((4,)), dma((4,)), dma((2,)), dma((2,)),
            dma((nz - 1,)), dma((nz - 1,)), dma((nz - 1,)), dma((nz - 1,)), dma((nz,)), dma((nz,)),
        ],
        compiler_params=pltpu.CompilerParams(
            collective_id=2, has_side_effects=True, vmem_limit_bytes=40 * 2**20
        ),
    )(
        grad.reshape(2, 2, ny, nz, part, width),
        rows.reshape(ny, nz, part, width),
        norm_gain.reshape(1, width),
    )
    return out


def body(pipe, vocab, hidden, norm_gain, out_weight, targets, loss_mask, slot_position, counts, loss_scale):
    micro_slots = hidden.shape[1]
    model_width = hidden.shape[2]
    shard_words = out_weight.shape[0]
    ny = 2
    nz = vocab // ny
    fast = pipe == 4 and vocab == ny * nz and nz <= 4 and micro_slots == 16 * vocab
    offset = lax.axis_index(("pipe", "vocab")) * shard_words
    own_rows = hidden.reshape(micro_slots, model_width).astype(F32)
    own_normed = rms_scale(own_rows, norm_gain).astype(BF16)
    own_ints = jnp.concatenate(
        [targets, loss_mask, slot_position, jnp.zeros((5, micro_slots), jnp.int32)], axis=0
    )
    if fast:
        all_normed, all_ints = gather(own_normed, own_ints, pipe, ny, 4)
    else:
        all_normed = lax.all_gather(own_normed, "pipe", axis=0, tiled=True)
        all_ints = lax.all_gather(own_ints, "pipe", axis=0)
    rows_total = all_normed.shape[0]
    all_targets, all_masks, all_positions = (
        all_ints[:, k].reshape(rows_total) for k in range(3)
    )
    count_row = jnp.broadcast_to(counts[:, None], (counts.shape[0], micro_slots)).reshape(rows_total)
    inside = all_positions < count_row
    token_weight = jnp.where(inside & (all_masks == 1), 1.0, 0.0).astype(F32)
    weight_total = jnp.sum(token_weight)
    logits = lax.dot_general(
        all_normed, out_weight, (((1,), (1,)), ((), ())), preferred_element_type=F32
    )
    is_target = (
        jnp.arange(shard_words, dtype=jnp.int32)[None, :] == (all_targets - offset)[:, None]
    )
    local_target = jnp.sum(jnp.where(is_target, logits, 0.0), axis=1)
    local_top = jnp.max(logits, axis=1)
    if fast:
        local_total = jnp.sum(jnp.exp(logits - local_top[:, None]), axis=1)
        log_total, target_logit = combine_stats(local_top, local_total, local_target, pipe, vocab)
    else:
        row_top = lax.pmax(local_top, ("pipe", "vocab"))
        local_total = jnp.sum(jnp.exp(logits - row_top[:, None]), axis=1)
        exp_total, target_logit = lax.psum((local_total, local_target), ("pipe", "vocab"))
        log_total = row_top + jnp.log(exp_total)
    loss = jnp.sum(token_weight * (log_total - target_logit)) / weight_total
    token_coef = loss_scale * token_weight / weight_total
    logit_grad = (
        (jnp.exp(logits - log_total[:, None]) - is_target.astype(F32)) * token_coef[:, None]
    ).astype(BF16)
    work_grad = jnp.dot(logit_grad, out_weight, preferred_element_type=F32)
    if fast:
        grad_out = reduce_finish(work_grad, hidden.reshape(micro_slots, model_width), norm_gain, ny, nz)
    else:
        grad_cube = work_grad.reshape(rows_total // micro_slots, micro_slots, model_width)
        micro_grad = lax.psum_scatter(grad_cube, "pipe", scatter_dimension=0, tiled=True)
        summed = lax.psum(micro_grad, "vocab")
        grad_out = pull_rows(own_rows, norm_gain, summed.reshape(micro_slots, model_width))
    return (loss, grad_out.reshape(1, micro_slots, model_width))


def solution(mesh):
    in_specs = (
        P("pipe", None, None),
        P(),
        P(("pipe", "vocab"), None),
        P("pipe", None),
        P("pipe", None),
        P("pipe", None),
        P(),
        P(),
    )
    out_specs = (P(), P("pipe", None, None))
    part = functools.partial(body, mesh.shape["pipe"], mesh.shape["vocab"])
    return jax.shard_map(part, mesh=mesh, in_specs=in_specs, out_specs=out_specs, check_vma=False)
```

time: 373 us -> 152 us (0.41)
  waiting for transfers between devices: 196 us -> 0 us
  blocking collectives: 96.8 us -> 0 us
  Pallas kernels: 0 us -> 87.1 us
  between operations: 16.9 us -> 3.87 us
  local copies, waits for them, and re-layouts: 0.1 us -> 4.96 us
  other arithmetic: 13.6 us -> 9.37 us
    psum x1 -> x0, waiting for transfers between devices: 105 us -> none  [body(): summed = lax.psum(micro_grad, 'vocab')]
    pallas_call x0 -> x3, Pallas kernels: none -> 87.1 us  [the longest x1 52.3 us: reduce_finish(): pl.pallas_call(functools.partial(reduce_kernel, ny, nz), out_shape=jax.Sh...]
    reduce_scatter x1 -> x0, waiting for transfers between devices: 71.2 us -> none  [body(): lax.psum_scatter(grad_cube, 'pipe', scatter_dimension=0, tiled=True)]
    psum x1 -> x0, blocking collectives: 41 us -> none  [softmax_stats(): lax.psum((local_total, local_target), ('pipe', 'vocab'))]
    pmax x1 -> x0, blocking collectives: 39.2 us -> none  [softmax_stats(): row_top = lax.pmax(jnp.max(logits, axis=1), ('pipe', 'vocab'))]
    all_gather x1 -> x0, waiting for transfers between devices: 19.9 us -> none  [body(): lax.all_gather(own_normed, 'pipe', axis=0, tiled=True)]
    all_gather x3 -> x0, blocking collectives: 16.6 us -> none  [the longest x1 6.01 us: body(): lax.all_gather(targets.reshape(micro_slots), 'pipe', axis=0, tiled=True)]
    reduce_sum x3 -> x1, other arithmetic: 6.71 us -> 2.16 us  [body(): local_total = jnp.sum(jnp.exp(logits - local_top[:, None]), axis=1)]
  transfers between devices with their start and end apart: 3 -> 0, of which waited for: 3 -> 0; matrix products, arithmetic and copies ran while one was open for 0% -> 0% of each run, Pallas kernels for 0% -> 0%
where the time goes in v1:
time: 152 us; the launch traced here: 151 us
  Pallas kernels  87.1 us (57%)
  matrix products  45.7 us (30%)
  other arithmetic  9.37 us (6%)
  local copies, waits for them, and re-layouts  4.96 us (3%)
  between operations  3.87 us (3%)
    pallas_call x1, Pallas kernels, reduce_finish(): pl.pallas_call(functools.partial(reduce_kernel, ny, nz), out_shape=jax.Sh...  52.3 us
    dot_general x1, matrix products, body(): work_grad = jnp.dot(logit_grad, out_weight, preferred_element_type=F32)  24.3 us
    pallas_call x1, Pallas kernels, gather(): pl.pallas_call(functools.partial(gather_kernel, ny, chunks), out_shape=(j...  22.1 us
    dot_general x1, matrix products, body(): lax.dot_general(all_normed, out_weight, (((1,), (1,)), ((), ())), preferr...  21.4 us
    pallas_call x1, Pallas kernels, combine_stats(): pl.pallas_call(functools.partial(stats_kernel, pipe, vocab), out_shape=ja...  12.6 us
    unnamed x9, local copies, waits for them, and re-layouts  4.12 us

profile of v1, /device:TPU:0, one launch (start us, length us, event | category | flops | bytes accessed | tf_op | source)
XLA Modules:
  0.0 151.0 jit_solution(9970715197166394369)
XLA Ops:
  1.3 1.5 %multiply_reduce_fusion = f32[128]{0:T(128)S(1)} fusion(bf16[1,128,4096]{2,1,0:T(8,128)(2,1)} %param.8), kind=kLoop, calls=%fused_computation.9 | loop fusion | flops 1572736 | bytes 1049088 | tf_op jit(solution)/shard_map/reduce_sum | solution.py:17
  2.8 0.1 pad.6.clone
  2.9 0.8 add_add_fusion.ints
  3.7 0.1 rsqrt.12
  3.7 1.6 %multiply_convert_fusion.2.own = bf16[2,4,16,4096]{3,2,1,0:T(8,128)(2,1)S(1)} fusion(bf16[2,4,16,4096]{3,2,1,0:T(8,128)(2,1)} %bitcast.30, f32[4096]{0:T(1024)} %param.9, f32[2,4,16]{2,1,0:T(4,128)S(1)} %rsqrt.12), kind=kLoop, calls=%fused_computation.8 | loop fusion | flops 2097152 | bytes 2114048 | tf_op jit(solution)/shard_map/convert_element_type | solution.py:308
  5.3 22.1 %shard_map.95 = (bf16[4,2,4,16,4096]{4,3,2,1,0:T(8,128)(2,1)S(1)}, s32[4,8,128]{2,1,0:T(8,128)S(1)}) custom-call(bf16[2,4,16,4096]{3,2,1,0:T(8,128)(2,1)S(1)} %multiply_convert_fusion.2.own, s32[8,128]{1,0:T(8,128)S(1)} %add_add_fusion.ints), custom_call_target="tpu_custom_call" | custom-call | tf_op jit(solution)/shard_map/pallas_call | solution.py:92
  27.5 0.7 compare_and_fusion
  28.2 21.4 %fusion.6 = (f32[512]{0:T(512)S(1)}, f32[512,4008]{0,1:T(8,128)S(1)}) fusion(bf16[512,4096]{1,0:T(8,128)(2,1)S(1)} %bitcast.35, bf16[4008,4096]{1,0:T(8,128)(2,1)} %param.10), kind=kOutput, calls=%fused_computation.23 | convolution fusion | flops 16812822528 | bytes 45238272 | tf_op jit(solution)/shard_map/dot_general | solution.py:325
  49.6 0.0 copy-start.2
  49.6 0.0 copy-start.3
  49.6 3.1 %copy-done.2 = f32[512,4008]{0,1:T(8,128)} copy-done((f32[512,4008]{0,1:T(8,128)}, f32[512,4008]{0,1:T(8,128)S(1)}, u32[]{:S(2)}) %copy-start.2) | copy-done | bytes 8208408
  52.8 2.2 %exponential_reduce_fusion = (f32[512]{0:T(512)S(1)}, f32[512]{0:T(512)S(1)}) fusion(f32[512,4008]{0,1:T(8,128)S(1)} %get-tuple-element.13, f32[512]{0:T(512)S(1)} %get-tuple-element.12, s32[512]{0:T(512)S(1)} %bitcast.36), kind=kLoop, calls=%fused_computation.3 | loop fusion | flops 10259456 | bytes 8216576 | tf_op jit(solution)/shard_map/reduce_sum | solution.py:334
  54.9 0.6 pad_maximum_fusion.st
  55.5 12.6 %shard_map.96 = f32[2,4,128]{2,1,0:T(4,128)} custom-call(f32[3,4,128]{2,1,0:T(4,128)} %pad_maximum_fusion.st), custom_call_target="tpu_custom_call" | custom-call | tf_op jit(solution)/shard_map/pallas_call | solution.py:147
  68.2 1.3 select_reduce_fusion.1
  70.8 0.0 copy-done.3
  70.8 0.7 multiply_divide_fusion
  71.5 0.7 slice_bitcast_fusion
  72.2 0.0 copy-start
  72.2 24.3 %fusion = f32[512,4096]{1,0:T(8,128)S(1)} fusion(bf16[4008,4096]{1,0:T(8,128)(2,1)} %param.10, f32[512,4008]{0,1:T(8,128)} %copy-done.2, f32[512]{0:T(512)S(1)} %multiply_divide_fusion, f32[512]{0:T(512)S(1)} %slice_bitcast_fusion, s32[512]{0:T(512)S(1)} %bitcast.37), kind=kOutput, calls=%fused_computation.4 | convolution fusion | flops 16823083008 | bytes 49436672 | tf_op jit(solution)/shard_map/dot_general | solution.py:346
  96.5 0.0 copy-done
  96.5 0.0 copy-done.1
  96.6 52.3 %shard_map.97 = bf16[2,4,16,4096]{3,2,1,0:T(8,128)(2,1)S(1)} custom-call(f32[2,2,2,4,16,4096]{5,4,3,2,1,0:T(8,128)S(1)} %bitcast.32, bf16[2,4,16,4096]{3,2,1,0:T(8,128)(2,1)S(1)} %bitcast.31, f32[1,4096]{1,0:T(1,128)S(1)} %bitcast.34), custom_call_target="tpu_custom_call" | custom-call | tf_op jit(solution)/shard_map/pallas_call | solution.py:267
  148.8 1.0 copy.14
  (5 shorter events, 0.0 us)
Async XLA Ops:
  49.6 3.2 %copy-start.2 = (f32[512,4008]{0,1:T(8,128)}, f32[512,4008]{0,1:T(8,128)S(1)}, u32[]{:S(2)}) copy-start(f32[512,4008]{0,1:T(8,128)S(1)} %get-tuple-element.13) | copy-start | bytes 24625156
  49.6 21.2 %copy-start.3 = (s32[4]{0:T(128)S(1)}, s32[4]{0:T(128)}, u32[]{:S(2)}) copy-start(s32[4]{0:T(128)} %param.14) | copy-start | bytes 52
  72.2 24.3 %copy-start = (bf16[1,128,4096]{2,1,0:T(8,128)(2,1)S(1)}, bf16[1,128,4096]{2,1,0:T(8,128)(2,1)}, u32[]{:S(2)}) copy-start(bf16[1,128,4096]{2,1,0:T(8,128)(2,1)} %param.8) | copy-start | bytes 3145732
  72.2 24.3 %copy-start.1 = (f32[4096]{0:T(1024)S(1)}, f32[4096]{0:T(1024)}, u32[]{:S(2)}) copy-start(f32[4096]{0:T(1024)} %param.9) | copy-start | bytes 49156
